TPU v7x, 256 devices: a whole 4x4x8 slice. The times are simulated.
256 devices in a mesh: bank: 8 (over z_lo, y), zero: 32 (over z_hi, x, core).
Axes of the slice: x: 4, y: 4, z: 8 (z_hi: 4, z_lo: 2; z = z_hi * 2 + z_lo), core: 2. Of those that a mesh axis runs over, the one named last changes fastest.
Arguments:
- train_down: float32 [16, 6400, 4096], P('bank', None, 'zero'), may hold values from -0.15625 to 0.15625
- other_down: bfloat16 [16, 6400, 4096], P('bank', None, 'zero'), may hold values from -0.0390625 to 0.0390625
- router_weight: float32 [4096, 16], P('zero', 'bank'), may hold values from -0.09375 to 0.09375
- router_gain: float32 [4096], P('zero'), may hold values from 0.25 to 1.75
Outputs:
- ready_down: bfloat16 [16, 6400, 4096], P('bank', 'zero')
- scale_down: float32 [16, 6400], P('bank', 'zero')
- serve_router: bfloat16 [4096, 16], replicated
All inputs are finite; a program needn't handle non-finite values. Where the computation divides by a largest or mean magnitude, that divisor is 1e-20 or more.
Results may differ from a plain program's by a relative error of at most 0.001.
Values may be sent and summed in bfloat16 or wider, within the bound.
A program may use at most 64 MiB of HBM per device.

v0:
```python
import jax
import jax.numpy as jnp
from jax import lax
from jax.sharding import PartitionSpec as P


def from_everyone(shard, axis):
    copies = jnp.broadcast_to(shard, (lax.axis_size(axis), *shard.shape))
    return lax.all_to_all(copies, axis, split_axis=0, concat_axis=0, tiled=True)


def taken_together(shard, axis):
    everything = from_everyone(shard, axis)
    return jnp.max(everything, axis=0)


def in_blocks(shard, dim, count):
    dims = shard.shape
    tiles = shard.reshape(*dims[:dim], count, dims[dim] // count, *dims[dim + 1 :])
    return jnp.moveaxis(tiles, dim, 0)


def piece_ends(length, count):
    unit = 8 if length >= 8 * count else 1
    return [length // unit * k // count * unit for k in range(1, count)]


def laid_out(tiles, dim):
    dims = list(tiles.shape[1:])
    dims[dim] *= tiles.shape[0]
    return jnp.moveaxis(tiles, 0, dim).reshape(dims)


def several_exchanges(shard, axis, pieces, split_dim, concat_dim):
    tiles = in_blocks(shard, split_dim, lax.axis_size(axis))
    cut = max(range(1, max(2, tiles.ndim - 1)), key=lambda d: tiles.shape[d])
    done = []
    for share in jnp.split(tiles, piece_ends(tiles.shape[cut], pieces), axis=cut):
        if share.size:
            done.append(lax.all_to_all(share, axis, split_axis=0, concat_axis=0, tiled=True))
    return laid_out(jnp.concatenate(done, axis=cut), concat_dim)


def gathered_copies(shard, axis, dim):
    tiles = from_everyone(shard, axis)
    return laid_out(tiles, dim)


def local(train_down, other_down, router_weight, router_gain):
    latest_down = train_down + other_down.astype(jnp.float32)
    scale_down = taken_together(jnp.max(jnp.abs(latest_down), axis=2), "zero")
    narrow_down = (latest_down / jnp.expand_dims(scale_down, 2)).astype(jnp.bfloat16)
    ready_down = several_exchanges(narrow_down, "zero", 2, 1, 2)
    scale_down = lax.dynamic_slice_in_dim(
        scale_down, lax.axis_index("zero") * ready_down.shape[1], ready_down.shape[1], axis=1
    )
    part_router = (router_weight * router_gain[:, None]).astype(jnp.bfloat16)
    row_router = gathered_copies(part_router, "zero", 0)
    serve_router = gathered_copies(row_router, "bank", 1)
    return (ready_down, scale_down, serve_router)


def solution(mesh):
    in_specs = (P("bank", None, "zero"), P("bank", None, "zero"), P("zero", "bank"), P("zero"))
    out_specs = (P("bank", "zero", None), P("bank", "zero"), P())
    return jax.shard_map(local, mesh=mesh, in_specs=in_specs, out_specs=out_specs, check_vma=False)
```

profile of v0, /device:TPU:41, one launch (start us, length us, event | category | flops | bytes accessed | tf_op | source)
XLA Modules:
  0.0 180.9 jit_solution(8569313873222200858)
XLA Ops:
  0.6 0.7 multiply_convert_fusion
  1.3 0.6 broadcast_in_dim.12
  1.9 10.9 %all-to-all-start.3 = ((bf16[32,128,2]{1,2,0:T(2,128)(2,1)}), bf16[32,128,2]{1,2,0:T(2,128)(2,1)S(1)}, u32[]{:S(2)}, u32[]{:S(2)}) async-start(bf16[32,128,2]{1,2,0:T(2,128)(2,1)} %broadcast_in_dim.12), calls=%async_computation.3 | async-start | bytes 32768 | tf_op jit(solution)/shard_map/all_to_all | solution.py:9
  12.8 5.6 %abs_reduce_fusion = f32[2,6400]{1,0:T(2,128)S(1)} fusion(f32[2,6400,128]{2,1,0:T(8,128)} %param.4, bf16[2,6400,128]{2,1,0:T(8,128)(2,1)} %param.5), kind=kLoop, calls=%fused_computation.1 | loop fusion | flops 6540800 | bytes 9881600 | tf_op jit(solution)/shard_map/reduce_max | solution.py:51
  18.4 3.7 %all-to-all-done.3 = bf16[32,128,2]{1,2,0:T(2,128)(2,1)S(1)} async-done(((bf16[32,128,2]{1,2,0:T(2,128)(2,1)}), bf16[32,128,2]{1,2,0:T(2,128)(2,1)S(1)}, u32[]{:S(2)}, u32[]{:S(2)}) %all-to-all-start.3) | async-done | bytes 16416 | tf_op jit(solution)/shard_map/all_to_all | solution.py:9
  22.1 0.4 broadcast_in_dim.11
  22.5 47.7 %all_to_all.25 = f32[32,2,6400]{2,1,0:T(2,128)S(1)} all-to-all(f32[32,2,6400]{2,1,0:T(2,128)S(1)} %broadcast_in_dim.11), channel_id=1, replica_groups=mesh['bank'=8,'zero'=32] {'zero'}, dimensions={0} | all-to-all | bytes 3276800 | tf_op jit(solution)/shard_map/all_to_all | solution.py:9
  70.2 0.7 broadcast_in_dim.13
  71.0 5.3 %all-to-all-start.4 = ((bf16[8,4096,2]{1,2,0:T(2,128)(2,1)}), bf16[8,4096,2]{1,2,0:T(2,128)(2,1)S(1)}, u32[]{:S(2)}, u32[]{:S(2)}) async-start(bf16[8,4096,2]{1,2,0:T(2,128)(2,1)} %broadcast_in_dim.13), calls=%async_computation.4 | async-start | bytes 262144 | tf_op jit(solution)/shard_map/all_to_all | solution.py:9
  76.2 0.6 reduce_max.19
  76.8 5.3 %divide_convert_fusion = bf16[2,6400,128]{2,1,0:T(8,128)(2,1)S(1)} fusion(f32[2,6400,128]{2,1,0:T(8,128)} %param.4, bf16[2,6400,128]{2,1,0:T(8,128)(2,1)} %param.5, f32[2,6400]{1,0:T(2,128)S(1)} %reduce_max.19), kind=kLoop, calls=%fused_computation | loop fusion | flops 6553600 | bytes 13158400 | tf_op jit(solution)/shard_map/convert_element_type | solution.py:52
  82.1 0.1 split.8
  82.2 1.3 copy.15
  83.6 0.0 all-to-all-done.4
  83.6 5.0 %all-to-all-start.1 = ((bf16[32,2,96,128]{3,2,1,0:T(8,128)(2,1)}), bf16[32,2,96,128]{3,2,1,0:T(8,128)(2,1)}, u32[]{:S(2)}, u32[]{:S(2)}) async-start(bf16[32,2,96,128]{3,2,1,0:T(8,128)(2,1)} %copy.15), calls=%async_computation.1 | async-start | bytes 3145728 | tf_op jit(solution)/shard_map/all_to_all | solution.py:40
  88.6 0.1 split.9
  88.7 1.3 copy.16
  90.1 39.3 %all-to-all-done.1 = bf16[32,2,96,128]{3,2,1,0:T(8,128)(2,1)} async-done(((bf16[32,2,96,128]{3,2,1,0:T(8,128)(2,1)}), bf16[32,2,96,128]{3,2,1,0:T(8,128)(2,1)}, u32[]{:S(2)}, u32[]{:S(2)}) %all-to-all-start.1) | async-done | bytes 1572896 | tf_op jit(solution)/shard_map/all_to_all | solution.py:40
  129.4 4.5 %all-to-all-start.2 = ((bf16[32,2,104,128]{3,2,1,0:T(8,128)(2,1)}), bf16[32,2,104,128]{3,2,1,0:T(8,128)(2,1)S(1)}, u32[]{:S(2)}, u32[]{:S(2)}) async-start(bf16[32,2,104,128]{3,2,1,0:T(8,128)(2,1)} %copy.16), calls=%async_computation.2 | async-start | bytes 3407872 | tf_op jit(solution)/shard_map/all_to_all | solution.py:40
  133.9 0.7 reshape.23
  134.6 0.7 constant_dynamic-slice_fusion
  135.2 42.1 %all-to-all-done.2 = bf16[32,2,104,128]{3,2,1,0:T(8,128)(2,1)S(1)} async-done(((bf16[32,2,104,128]{3,2,1,0:T(8,128)(2,1)}), bf16[32,2,104,128]{3,2,1,0:T(8,128)(2,1)S(1)}, u32[]{:S(2)}, u32[]{:S(2)}) %all-to-all-start.2) | async-done | bytes 1703968 | tf_op jit(solution)/shard_map/all_to_all | solution.py:40
  177.3 3.6 %copy_bitcast_fusion = bf16[2,200,4096]{2,1,0:T(8,128)(2,1)} fusion(bf16[32,2,104,128]{3,2,1,0:T(8,128)(2,1)S(1)} %all-to-all-done.2, bf16[32,2,96,128]{3,2,1,0:T(8,128)(2,1)} %all-to-all-done.1), kind=kLoop, calls=%fused_computation.3 | loop fusion | flops 6553600 | bytes 6553600 | tf_op jit(solution)/shard_map/reshape | solution.py:31
Async XLA Ops:
  1.9 20.2 %all-to-all-start.3 = ((bf16[32,128,2]{1,2,0:T(2,128)(2,1)}), bf16[32,128,2]{1,2,0:T(2,128)(2,1)S(1)}, u32[]{:S(2)}, u32[]{:S(2)}) async-start(bf16[32,128,2]{1,2,0:T(2,128)(2,1)} %broadcast_in_dim.12), calls=%async_computation.3 | async-start | bytes 32768 | tf_op jit(solution)/shard_map/all_to_all | solution.py:9
  71.0 12.6 %all-to-all-start.4 = ((bf16[8,4096,2]{1,2,0:T(2,128)(2,1)}), bf16[8,4096,2]{1,2,0:T(2,128)(2,1)S(1)}, u32[]{:S(2)}, u32[]{:S(2)}) async-start(bf16[8,4096,2]{1,2,0:T(2,128)(2,1)} %broadcast_in_dim.13), calls=%async_computation.4 | async-start | bytes 262144 | tf_op jit(solution)/shard_map/all_to_all | solution.py:9
  83.6 45.8 %all-to-all-start.1 = ((bf16[32,2,96,128]{3,2,1,0:T(8,128)(2,1)}), bf16[32,2,96,128]{3,2,1,0:T(8,128)(2,1)}, u32[]{:S(2)}, u32[]{:S(2)}) async-start(bf16[32,2,96,128]{3,2,1,0:T(8,128)(2,1)} %copy.15), calls=%async_computation.1 | async-start | bytes 3145728 | tf_op jit(solution)/shard_map/all_to_all | solution.py:40
  129.4 47.9 %all-to-all-start.2 = ((bf16[32,2,104,128]{3,2,1,0:T(8,128)(2,1)}), bf16[32,2,104,128]{3,2,1,0:T(8,128)(2,1)S(1)}, u32[]{:S(2)}, u32[]{:S(2)}) async-start(bf16[32,2,104,128]{3,2,1,0:T(8,128)(2,1)} %copy.16), calls=%async_computation.2 | async-start | bytes 3407872 | tf_op jit(solution)/shard_map/all_to_all | solution.py:40
where the time goes:
time: 181 us
  waiting for transfers between devices  85.1 us (47%)
  blocking collectives  47.7 us (26%)
  starting transfers between devices  25.6 us (14%)
  other arithmetic  15.8 us (9%)
  local copies, waits for them, and re-layouts  6.02 us (3%)
    all_to_all x2, waiting for transfers between devices, several_exchanges(): lax.all_to_all(share, axis, split_axis=0, concat_axis=0, tiled=True)  81.4 us
    all_to_all x1, blocking collectives, from_everyone(): return lax.all_to_all(copies, axis, split_axis=0, concat_axis=0, tiled=True)  47.7 us
    all_to_all x2, starting transfers between devices, from_everyone(): return lax.all_to_all(copies, axis, split_axis=0, concat_axis=0, tiled=True)  16.1 us
    all_to_all x2, starting transfers between devices, several_exchanges(): lax.all_to_all(share, axis, split_axis=0, concat_axis=0, tiled=True)  9.49 us
    reduce_max x1, other arithmetic, local(): scale_down = taken_together(jnp.max(jnp.abs(latest_down), axis=2), 'zero')  5.6 us
    convert_element_type x1, other arithmetic, local(): (latest_down / jnp.expand_dims(scale_down, 2)).astype(jnp.bfloat16)  5.32 us
    all_to_all x2, waiting for transfers between devices, from_everyone(): return lax.all_to_all(copies, axis, split_axis=0, concat_axis=0, tiled=True)  3.7 us
  transfers between devices with their start and end apart: 4, of which 3 were waited for; matrix products, arithmetic and copies ran while one was open for 9% of the time, Pallas kernels for 0%

commit v1 on v0

v1 whole, which is shorter than its diff:
```python
import functools

import jax
import jax.numpy as jnp
from jax import lax
from jax.experimental import pallas as pl
from jax.experimental.pallas import tpu as pltpu
from jax.sharding import PartitionSpec as P

MESH = pl.DeviceIdType.MESH
CHUNKS = 8
SUB, LANES = 8, 128


def remote(src, dst, send, recv, where):
    return pltpu.make_async_remote_copy(
        src_ref=src, dst_ref=dst, send_sem=send, recv_sem=recv, device_id=where, device_id_type=MESH
    )


def kernel(
    n, banks, train, other, weight, gain, ready, scale, serve,
    x_buf, o_buf, part, heard, told, inv, sent, r_in, r_out,
    in_sem, max_send, max_recv, inv_send, inv_recv, row_send, row_recv, rt_send, rt_recv, rt_own, send_sem, recv_sem, own_sem,
):
    me, bank = lax.axis_index("zero"), lax.axis_index("bank")
    experts, _, rows, _ = x_buf.shape
    tiles = rows // SUB
    per = n // CHUNKS
    lane = lax.broadcasted_iota(jnp.int32, (SUB, LANES), 1)
    row = lax.broadcasted_iota(jnp.int32, (SUB, LANES), 0)

    barrier = pltpu.get_barrier_semaphore()

    def load(g):
        at = pl.ds(g * per, per)
        return (
            pltpu.make_async_copy(train.at[:, at], x_buf.at[:, at], in_sem.at[0, g]),
            pltpu.make_async_copy(other.at[:, at], o_buf.at[:, at], in_sem.at[1, g]),
        )

    for g in range(CHUNKS):
        for copy in load(g):
            copy.start()

    @pl.loop(1, n)
    def _(k):
        pl.semaphore_signal(barrier, inc=1, device_id={"zero": lax.rem(me + k, n)}, device_id_type=MESH)

    @pl.loop(1, banks)
    def _(k):
        pl.semaphore_signal(barrier, inc=1, device_id={"bank": lax.rem(bank + k, banks)}, device_id_type=MESH)

    mine = (weight[...] * gain[...]).astype(jnp.bfloat16).astype(jnp.float32)
    r_in[bank] = mine

    @pl.loop(0, CHUNKS)
    def _(g):
        for copy in load(g):
            copy.wait()

        @pl.loop(g * per, g * per + per)
        def _(d):
            tile = jnp.zeros((SUB, LANES), jnp.float32)
            for e in range(experts):
                x = x_buf[e, d] + o_buf[e, d].astype(jnp.float32)
                x_buf[e, d] = x
                top = jnp.max(jnp.abs(x).reshape(tiles, SUB, LANES), axis=2, keepdims=True)
                for t in range(tiles):
                    tile = jnp.where(lane == e * tiles + t, top[t], tile)
            part[d] = tile

    pl.semaphore_wait(barrier, n - 1 + banks - 1)

    def to_owner(d):
        return remote(part.at[d], heard.at[me], max_send.at[d], max_recv.at[me], {"zero": d})

    @pl.loop(1, n)
    def _(k):
        to_owner(lax.rem(me + k, n)).start()

    def to_bank(b):
        return remote(r_in.at[bank], r_in.at[bank], row_send.at[b], row_recv.at[bank], {"bank": b})

    @pl.loop(1, banks)
    def _(k):
        to_bank(lax.rem(bank + k, banks)).start()

    heard[me] = part[me]

    @pl.loop(1, n)
    def _(k):
        s = lax.rem(me + k, n)
        remote(part.at[s], heard.at[s], max_send.at[s], max_recv.at[s], {"zero": s}).wait_recv()

    top = heard[0]
    for s in range(1, n):
        top = jnp.maximum(top, heard[s])
    used = lane < experts * tiles
    told[0] = jnp.where(used, 1.0 / jnp.where(used, top, 1.0), 0.0)

    for e in range(experts):
        for first in range(0, rows, LANES):
            width = min(LANES, rows - first)
            line = jnp.zeros((SUB, LANES), jnp.float32)
            for t in range(first // SUB, (first + width) // SUB):
                c = e * tiles + t
                column = jnp.broadcast_to(top[:, c : c + 1], (SUB, LANES))
                line = jnp.where(lane == t * SUB - first + row, column, line)
            scale[e : e + 1, first : first + width] = jnp.max(line, axis=0, keepdims=True)[:, :width]

    def to_all(d):
        return remote(told.at[0], inv.at[me], inv_send.at[d], inv_recv.at[me], {"zero": d})

    @pl.loop(1, n)
    def _(k):
        to_all(lax.rem(me + k, n)).start()

    inv[me] = told[0]

    def piece(d, at):
        return ready.at[:, :, pl.ds(pl.multiple_of(at * LANES, LANES), LANES)]

    def narrow(d):
        factor = inv[d]
        for e in range(experts):
            wide = [jnp.broadcast_to(factor[:, e * tiles + t : e * tiles + t + 1], (SUB, LANES)) for t in range(tiles)]
            sent[d, e] = (x_buf[e, d] * jnp.concatenate(wide, axis=0)).astype(jnp.bfloat16)

    def to_server(d):
        return remote(sent.at[d], piece(d, me), send_sem.at[d], recv_sem.at[me], {"zero": d})

    @pl.loop(1, n + 1)
    def _(k):
        @pl.when(k < n)
        def _():
            d = lax.rem(me + k, n)
            remote(told.at[0], inv.at[d], inv_send.at[d], inv_recv.at[d], {"zero": d}).wait_recv()
            narrow(d)

        @pl.when(k > 1)
        def _():
            to_server(lax.rem(me + k - 1, n)).start()

    narrow(me)

    @pl.loop(1, banks)
    def _(k):
        b = lax.rem(bank + k, banks)
        remote(r_in.at[b], r_in.at[b], row_send.at[b], row_recv.at[b], {"bank": b}).wait_recv()

    r_out[...] = jnp.concatenate([r_in[b] for b in range(banks)], axis=0).astype(jnp.bfloat16)

    own = pltpu.make_async_copy(sent.at[me], piece(me, me), own_sem)
    own.start()

    def lines(at):
        return serve.at[:, pl.ds(pl.multiple_of(at * LANES, LANES), LANES)]

    @pl.loop(1, n)
    def _(k):
        d = lax.rem(me + k, n)
        remote(r_out, lines(me), rt_send.at[d], rt_recv.at[me], {"zero": d}).start()

    kept = pltpu.make_async_copy(r_out, lines(me), rt_own)
    kept.start()

    own.wait()
    kept.wait()

    @pl.loop(1, n)
    def _(k):
        d = lax.rem(me + k, n)
        to_owner(d).wait_send()
        to_all(d).wait_send()

    @pl.loop(1, banks)
    def _(k):
        to_bank(lax.rem(bank + k, banks)).wait_send()

    @pl.loop(1, n)
    def _(k):
        d = lax.rem(me + k, n)
        remote(r_out, lines(d), rt_send.at[d], rt_recv.at[d], {"zero": d}).wait()
        remote(sent.at[d], piece(d, d), send_sem.at[d], recv_sem.at[d], {"zero": d}).wait()


def solution(mesh):
    n, banks = mesh.shape["zero"], mesh.shape["bank"]

    def local(train_down, other_down, router_weight, router_gain):
        experts, length, width = train_down.shape
        rows = length // n
        split = (experts, n, rows, width)
        dma = pltpu.SemaphoreType.DMA
        ready, scale, serve = pl.pallas_call(
            functools.partial(kernel, n, banks),
            out_shape=(
                jax.ShapeDtypeStruct((experts, rows, n * width), jnp.bfloat16),
                jax.ShapeDtypeStruct((experts, rows), jnp.float32),
                jax.ShapeDtypeStruct((banks * experts, n * width), jnp.bfloat16),
            ),
            in_specs=[pl.BlockSpec(memory_space=pltpu.HBM)] * 2 + [pl.BlockSpec(memory_space=pltpu.VMEM)] * 2,
            out_specs=(
                pl.BlockSpec(memory_space=pl.ANY),
                pl.BlockSpec(memory_space=pltpu.VMEM),
                pl.BlockSpec(memory_space=pl.ANY),
            ),
            scratch_shapes=[
                pltpu.VMEM(split, jnp.float32),
                pltpu.VMEM(split, jnp.bfloat16),
                pltpu.VMEM((n, SUB, LANES), jnp.float32),
                pltpu.VMEM((n, SUB, LANES), jnp.float32),
                pltpu.VMEM((1, SUB, LANES), jnp.float32),
                pltpu.VMEM((n, SUB, LANES), jnp.float32),
                pltpu.VMEM((n, experts, rows, width), jnp.bfloat16),
                pltpu.VMEM((banks, experts, width), jnp.float32),
                pltpu.VMEM((banks * experts, width), jnp.bfloat16),
                dma((2, CHUNKS)),
                dma((n,)), dma((n,)), dma((n,)), dma((n,)),
                dma((banks,)), dma((banks,)),
                dma((n,)), dma((n,)), dma,
                dma((n,)), dma((n,)), dma,
            ],
            compiler_params=pltpu.CompilerParams(
                collective_id=0, has_side_effects=True, vmem_limit_bytes=56 * 1024 * 1024
            ),
        )(
            train_down.reshape(split),
            other_down.reshape(split),
            router_weight.T,
            router_gain[None, :],
        )
        return ready, scale, serve.T

    in_specs = (P("bank", None, "zero"), P("bank", None, "zero"), P("zero", "bank"), P("zero"))
    out_specs = (P("bank", "zero", None), P("bank", "zero"), P())
    return jax.shard_map(local, mesh=mesh, in_specs=in_specs, out_specs=out_specs, check_vma=False)
```

time: 181 us -> 133 us (0.73)
  the two profiles are of different devices: /device:TPU:41 before, /device:TPU:97 now
where the time goes in v1:
time: 133 us
  Pallas kernels  127 us (95%)
  local copies, waits for them, and re-layouts  5.28 us (4%)
    pallas_call x1, Pallas kernels, local(): pl.pallas_call(functools.partial(kernel, n, banks), out_shape=(jax.ShapeD...  127 us
    unnamed x7, local copies, waits for them, and re-layouts  5.28 us

profile of v1, /device:TPU:97, one launch (start us, length us, event | category | flops | bytes accessed | tf_op | source)
XLA Modules:
  0.0 133.3 jit_solution(8422759397606535802)
XLA Ops:
  0.6 127.4 %shard_map.67 = (bf16[2,200,4096]{2,1,0:T(8,128)(2,1)}, f32[2,200]{1,0:T(2,128)}, bf16[16,4096]{1,0:T(8,128)(2,1)}) custom-call(f32[2,32,200,128]{3,2,1,0:T(8,128)} %bitcast.5, bf16[2,32,200,128]{3,2,1,0:T(8,128)(2,1)} %bitcast.6, f32[2,128]{1,0:T(2,128)} %bitcast.8, f32[1,128]{1,0:T(1,128)} %bitcast.9), custom_call_target="tpu_custom_call" | custom-call | tf_op jit(solution)/shard_map/pallas_call | solution.py:196
  128.0 0.0 copy-start.1
  128.0 0.0 copy-start
  128.0 4.0 %copy.10 = bf16[2,200,4096]{2,1,0:T(8,128)(2,1)} copy(bf16[2,200,4096]{2,1,0:T(8,128)(2,1)} %get-tuple-element.12) | data formatting | bytes 6553600
  132.1 0.0 copy-done.1
  132.1 0.6 copy.11
  132.7 0.0 copy-done
  132.7 0.7 copy.12
Async XLA Ops:
  128.0 4.1 %copy-start.1 = (f32[2,200]{1,0:T(2,128)S(1)}, f32[2,200]{1,0:T(2,128)}, u32[]{:S(2)}) copy-start(f32[2,200]{1,0:T(2,128)} %get-tuple-element.13) | copy-start | bytes 4804
  128.0 4.6 %copy-start = (bf16[16,4096]{1,0:T(8,128)(2,1)S(1)}, bf16[16,4096]{1,0:T(8,128)(2,1)}, u32[]{:S(2)}) copy-start(bf16[16,4096]{1,0:T(8,128)(2,1)} %get-tuple-element.8) | copy-start | bytes 393220

commit v2 on v1

--- a/solution.py
+++ b/solution.py
@@ -30,6 +30,17 @@
     lane = lax.broadcasted_iota(jnp.int32, (SUB, LANES), 1)
     row = lax.broadcasted_iota(jnp.int32, (SUB, LANES), 0)
 
+
+    def peer(k):
+        k = k - 1
+        far = k < 24
+        i = jnp.where(far, k // 3, k - 23)
+        j = k % 3
+        dz = jnp.where(far, jnp.where(j == 0, 1, jnp.where(j == 1, 3, 2)), 0)
+        dx, dc = i // 2, i % 2
+        z, x, c = (me // 8 + dz) % 4, (me // 2 + dx) % 4, (me + dc) % 2
+        return z * 8 + x * 2 + c
+
     barrier = pltpu.get_barrier_semaphore()
 
     def load(g):
@@ -45,7 +56,7 @@
 
     @pl.loop(1, n)
     def _(k):
-        pl.semaphore_signal(barrier, inc=1, device_id={"zero": lax.rem(me + k, n)}, device_id_type=MESH)
+        pl.semaphore_signal(barrier, inc=1, device_id={"zero": peer(k)}, device_id_type=MESH)
 
     @pl.loop(1, banks)
     def _(k):
@@ -77,7 +88,7 @@
 
     @pl.loop(1, n)
     def _(k):
-        to_owner(lax.rem(me + k, n)).start()
+        to_owner(peer(k)).start()
 
     def to_bank(b):
         return remote(r_in.at[bank], r_in.at[bank], row_send.at[b], row_recv.at[bank], {"bank": b})
@@ -90,7 +101,7 @@
 
     @pl.loop(1, n)
     def _(k):
-        s = lax.rem(me + k, n)
+        s = peer(k)
         remote(part.at[s], heard.at[s], max_send.at[s], max_recv.at[s], {"zero": s}).wait_recv()
 
     top = heard[0]
@@ -114,7 +125,7 @@
 
     @pl.loop(1, n)
     def _(k):
-        to_all(lax.rem(me + k, n)).start()
+        to_all(peer(k)).start()
 
     inv[me] = told[0]
 
@@ -134,13 +145,13 @@
     def _(k):
         @pl.when(k < n)
         def _():
-            d = lax.rem(me + k, n)
+            d = peer(k)
             remote(told.at[0], inv.at[d], inv_send.at[d], inv_recv.at[d], {"zero": d}).wait_recv()
             narrow(d)
 
         @pl.when(k > 1)
         def _():
-            to_server(lax.rem(me + k - 1, n)).start()
+            to_server(peer(k - 1)).start()
 
     narrow(me)
 
@@ -159,7 +170,7 @@
 
     @pl.loop(1, n)
     def _(k):
-        d = lax.rem(me + k, n)
+        d = peer(k)
         remote(r_out, lines(me), rt_send.at[d], rt_recv.at[me], {"zero": d}).start()
 
     kept = pltpu.make_async_copy(r_out, lines(me), rt_own)
@@ -170,7 +181,7 @@
 
     @pl.loop(1, n)
     def _(k):
-        d = lax.rem(me + k, n)
+        d = peer(k)
         to_owner(d).wait_send()
         to_all(d).wait_send()
 
@@ -180,7 +191,7 @@
 
     @pl.loop(1, n)
     def _(k):
-        d = lax.rem(me + k, n)
+        d = peer(k)
         remote(r_out, lines(d), rt_send.at[d], rt_recv.at[d], {"zero": d}).wait()
         remote(sent.at[d], piece(d, d), send_sem.at[d], recv_sem.at[d], {"zero": d}).wait()
 
@@ -223,7 +234,7 @@
                 dma((n,)), dma((n,)), dma,
             ],
             compiler_params=pltpu.CompilerParams(
-                collective_id=0, has_side_effects=True, vmem_limit_bytes=56 * 1024 * 1024
+                collective_id=0, has_side_effects=True, vmem_limit_bytes=48 * 1024 * 1024
             ),
         )(
             train_down.reshape(split),

time: 133 us -> 108 us (0.81)
  the two profiles are of different devices: /device:TPU:97 before, /device:TPU:41 now
where the time goes in v2:
time: 108 us; the launch traced here: 107 us
  Pallas kernels  102 us (94%)
  local copies, waits for them, and re-layouts  4.27 us (4%)
    pallas_call x1, Pallas kernels, local(): pl.pallas_call(functools.partial(kernel, n, banks), out_shape=(jax.ShapeD...  102 us
    unnamed x7, local copies, waits for them, and re-layouts  4.27 us

profile of v2, /device:TPU:41, one launch (start us, length us, event | category | flops | bytes accessed | tf_op | source)
XLA Modules:
  0.0 106.9 jit_solution(2761279574459798883)
XLA Ops:
  0.6 0.0 copy-start
  0.6 0.7 copy-done
  1.3 0.0 copy-start.1
  1.3 0.7 copy-done.1
  2.0 102.0 %shard_map.67 = (bf16[2,200,4096]{2,1,0:T(8,128)(2,1)S(1)}, f32[2,200]{1,0:T(2,128)S(1)}, bf16[16,4096]{1,0:T(8,128)(2,1)S(1)}) custom-call(f32[2,32,200,128]{3,2,1,0:T(8,128)} %bitcast.8, bf16[2,32,200,128]{3,2,1,0:T(8,128)(2,1)} %bitcast.9, f32[2,128]{1,0:T(2,128)S(1)} %bitcast.6, f32[1,128]{1,0:T(1,128)S(1)} %bitcast.7), custom_call_target="tpu_custom_call" | custom-call | tf_op jit(solution)/shard_map/pallas_call | solution.py:207
  104.0 1.7 %copy.10 = bf16[2,200,4096]{2,1,0:T(8,128)(2,1)} copy(bf16[2,200,4096]{2,1,0:T(8,128)(2,1)S(1)} %get-tuple-element.12) | data formatting | bytes 6553600
  105.7 0.6 copy.11
  106.2 0.7 copy.12
Async XLA Ops:
  0.6 0.7 copy-start
  1.3 0.7 copy-start.1

commit v3 on v0

v3 whole, which is shorter than its diff:
```python
import functools

import jax
import jax.numpy as jnp
from jax import lax
from jax.experimental import pallas as pl
from jax.experimental.pallas import tpu as pltpu
from jax.sharding import PartitionSpec as P

MESH = pl.DeviceIdType.MESH
SUB, LANES = 8, 128
HALF = SUB // 2
PLANES = 4
CHUNKS = 8
UNIT = 40
SLABS = 2
EARLY, PACE = 6, 1
DURING = 6


def remote(src, dst, send, recv, where):
    return pltpu.make_async_remote_copy(
        src_ref=src, dst_ref=dst, send_sem=send, recv_sem=recv, device_id=where, device_id_type=MESH
    )


def kernel(
    n, banks, train, other, weight, gain, ready, scale, serve,
    x_buf, o_buf, w_buf, g_buf, loose, part, heard, told, inv, sent, lines, raw_in,
    in_sem, max_send, max_recv, inv_send, inv_recv, row_send, row_recv, line_send, line_recv,
    send_sem, recv_sem, own_sem, raw_send, raw_recv,
):
    me, bank = lax.axis_index("zero"), lax.axis_index("bank")
    experts, _, rows, _ = x_buf.shape
    tiles, units = rows // SUB, rows // UNIT
    per, plane = n // CHUNKS, n // PLANES
    lane = lax.broadcasted_iota(jnp.int32, (SUB, LANES), 1)
    row = lax.broadcasted_iota(jnp.int32, (SUB, LANES), 0)

    def peer(up, i):
        z, x, c = lax.rem(me // plane + up, PLANES), lax.rem(me % plane // 2 + i // 2, plane // 2), lax.rem(me + i, 2)
        return z * plane + x * 2 + c

    def back(up, i):
        z, x, c = lax.rem(me // plane + PLANES - up, PLANES), lax.rem(me % plane // 2 + plane // 2 - i // 2, plane // 2), lax.rem(me + i, 2)
        return z * plane + x * 2 + c

    half = lax.broadcasted_iota(jnp.int32, (HALF, LANES), 1)

    def packed(tile):
        return jnp.where(half < LANES // 2, tile[:HALF], pltpu.roll(tile[HALF:], LANES // 2, 1))

    def spread(tile):
        return jnp.concatenate([tile, pltpu.roll(tile, LANES // 2, 1)], axis=0)

    def others(body, ups=(2, 1, 3, 0)):
        for up in ups:

            @pl.loop(1 if up == 0 else 0, plane)
            def _(i):
                body(peer(up, i))

    def chunk(k):
        return lax.rem(me // per + plane // per + k, CHUNKS)

    def load(k):
        g = chunk(k)
        at = pl.ds(g * per, per)
        return (
            pltpu.make_async_copy(train.at[:, at], x_buf.at[:, at], in_sem.at[0, g]),
            pltpu.make_async_copy(other.at[:, at], o_buf.at[:, at], in_sem.at[1, g]),
        )

    small = (
        pltpu.make_async_copy(weight, w_buf, in_sem.at[0, CHUNKS]),
        pltpu.make_async_copy(gain, g_buf, in_sem.at[1, CHUNKS]),
    )
    barrier = pltpu.get_barrier_semaphore()
    for k in range(CHUNKS):
        for copy in load(k):
            copy.start()
    others(lambda d: pl.semaphore_signal(barrier, inc=1, device_id={"zero": d}, device_id_type=MESH))
    for copy in small:
        copy.start()

    across = lax.rem(bank + banks // 2, banks)
    row_of = banks // 2
    beside = [bank // row_of * row_of + lax.rem(bank + k, row_of) for k in range(1, row_of)]
    for b in [across] + beside:
        pl.semaphore_signal(barrier, inc=1, device_id={"bank": b}, device_id_type=MESH)

    def raw(way, u):
        slab, unit = u // units, u % units
        e, i = slab % experts, slab // experts
        d, at = peer(1 + 2 * way, i), pl.ds(unit * UNIT, UNIT)
        return remote(x_buf.at[e, d, at], raw_in.at[way, slab, at], raw_send.at[way, u], raw_recv.at[way, u], {"zero": d})

    def raws(first, last):
        for u in range(first, last):
            for way in range(2):
                raw(way, u).start()

    def maxima(k):
        for copy in load(k):
            copy.wait()
        for j in range(per):
            d = chunk(k) * per + j
            tile = jnp.zeros((SUB, LANES), jnp.float32)
            for e in range(experts):
                x = x_buf[e, d] + o_buf[e, d].astype(jnp.float32)
                x_buf[e, d] = x
                top = jnp.max(jnp.abs(x).reshape(tiles, SUB, LANES), axis=2, keepdims=True)
                for t in range(tiles):
                    tile = jnp.where(lane == e * tiles + t, top[t], tile)
            loose[d] = tile

    pl.loop(0, EARLY)(maxima)
    pl.semaphore_wait(barrier, n - 1 + row_of)

    @pl.loop(EARLY, CHUNKS)
    def _(g):
        maxima(g)
        for way in range(2):
            for k in range(PACE):
                raw(way, (g - EARLY) * PACE + k).start()

    for d in range(n):
        part[d] = packed(loose[d])

    def to_owner(d):
        return remote(part.at[d], heard.at[me], max_send.at[d], max_recv.at[me], {"zero": d})

    others(lambda d: to_owner(d).start())

    raws((CHUNKS - EARLY) * PACE, (CHUNKS - EARLY) * PACE + DURING)

    for copy in small:
        copy.wait()
    lines[bank, me] = (w_buf[...] * g_buf[...]).astype(jnp.bfloat16).astype(jnp.float32)

    def to_rows(d):
        return remote(lines.at[bank, me], lines.at[bank, me], row_send.at[d], row_recv.at[me], {"zero": d})

    def from_rows(s):
        remote(lines.at[bank, s], lines.at[bank, s], row_send.at[s], row_recv.at[s], {"zero": s}).wait_recv()

    def line(at, to, k):
        return remote(lines.at[at], lines.at[at], line_send.at[k], line_recv.at[k], {"bank": to})

    others(lambda d: to_rows(d).start())

    heard[me] = part[me]

    @pl.loop(0, n)
    def _(s):
        @pl.when(s != me)
        def _():
            remote(part.at[s], heard.at[s], max_send.at[s], max_recv.at[s], {"zero": s}).wait_recv()

    top = heard[0]
    for s in range(1, n):
        top = jnp.maximum(top, heard[s])
    used = lax.rem(half, LANES // 2) < experts * tiles
    told[0] = jnp.where(used, 1.0 / jnp.where(used, top, 1.0), 0.0)
    top = spread(top)

    def to_all(d):
        return remote(told.at[0], inv.at[me], inv_send.at[d], inv_recv.at[me], {"zero": d})

    others(lambda d: to_all(d).start(), (1, 3, 2, 0))

    raws((CHUNKS - EARLY) * PACE + DURING, SLABS * units)

    def piece(e, at):
        return ready.at[e, :, pl.ds(pl.multiple_of(at * LANES, LANES), LANES)]

    def narrow(d, e, source, factor):
        factor = spread(factor)
        wide = [jnp.broadcast_to(factor[:, e * tiles + t : e * tiles + t + 1], (SUB, LANES)) for t in range(tiles)]
        sent[d, e] = (source * jnp.concatenate(wide, axis=0)).astype(jnp.bfloat16)

    def to_server(d, e):
        return remote(sent.at[d, e], piece(e, me), send_sem.at[d, e], recv_sem.at[me, e], {"zero": d})

    def known(d):
        remote(told.at[0], inv.at[d], inv_send.at[d], inv_recv.at[d], {"zero": d}).wait_recv()

    def step(up, i, was):
        d = peer(up, i)
        known(d)
        for e in range(experts):
            narrow(d, e, x_buf[e, d], inv[d])
        for e in range(experts):
            to_server(was, e).start()
        return d

    halves = [(peer(up, slab // experts), slab % experts) for slab in range(SLABS, -(-SLABS // experts) * experts) for up in (1, 3)]
    whole = -(-SLABS // experts)
    for up in (1, 3):
        for i in range(whole):
            known(peer(up, i))
    for d, e in halves:
        narrow(d, e, x_buf[e, d], inv[d])
    was = peer(1, whole)
    known(was)
    for e in range(experts):
        narrow(was, e, x_buf[e, was], inv[was])
    for d, e in halves:
        to_server(d, e).start()
    was = step(3, whole, was)

    @pl.loop(0, n)
    def _(s):
        @pl.when(s != me)
        def _():
            from_rows(s)

    line(bank, across, 0).start()

    was = lax.fori_loop(whole + 1, 4, lambda i, was: step(3, i, step(1, i, was)), was)

    line(bank, across, 0).wait()
    for k, b in enumerate(beside):
        line(bank, b, 1 + k).start()
        line(across, b, row_of + k).start()

    was = lax.fori_loop(0, 4, lambda i, was: step(2, i, was), was)
    was = lax.fori_loop(4, plane, lambda i, was: step(2, i, step(3, i, step(1, i, was))), was)
    was = lax.fori_loop(1, plane, lambda i, was: step(0, i, was), was)
    for e in range(experts):
        to_server(was, e).start()

    for e in range(experts):
        narrow(me, e, x_buf[e, me], told[0])
    local = [pltpu.make_async_copy(sent.at[me, e], piece(e, me), own_sem.at[e]) for e in range(experts)]
    for copy in local:
        copy.start()
    for slab in range(SLABS):
        e, i = slab % experts, slab // experts
        for way in range(2):
            slot, source = peer(1 + 2 * way, i), back(1 + 2 * way, i)
            for u in range(slab * units, slab * units + units):
                raw(way, u).wait()
            narrow(slot, e, raw_in[way, slab], told[0])
            local.append(pltpu.make_async_copy(sent.at[slot, e], piece(e, source), own_sem.at[experts + 2 * slab + way]))
            local[-1].start()

    for e in range(experts):
        for first in range(0, rows, LANES):
            width = min(LANES, rows - first)
            strip = jnp.zeros((SUB, LANES), jnp.float32)
            for t in range(first // SUB, (first + width) // SUB):
                c = e * tiles + t
                column = jnp.broadcast_to(top[:, c : c + 1], (SUB, LANES))
                strip = jnp.where(lane == t * SUB - first + row, column, strip)
            scale[e : e + 1, first : first + width] = jnp.max(strip, axis=0, keepdims=True)[:, :width]

    for copy in local:
        copy.wait()
    for k in range(1, row_of):
        b = bank // row_of * row_of + lax.rem(bank + row_of - k, row_of)
        far = lax.rem(b + banks // 2, banks)
        line(bank, beside[k - 1], k).wait_send()
        line(across, beside[k - 1], row_of + k - 1).wait_send()
        remote(lines.at[b], lines.at[b], line_send.at[k], line_recv.at[k], {"bank": b}).wait_recv()
        remote(lines.at[far], lines.at[far], line_send.at[row_of + k - 1], line_recv.at[row_of + k - 1], {"bank": b}).wait_recv()
    for s in range(n):
        columns = jnp.concatenate([lines[b, s] for b in range(banks)], axis=0)
        serve[:, s * LANES : (s + 1) * LANES] = columns.astype(jnp.bfloat16)

    gone = [peer(up, i) for i in range(whole) for up in (1, 3)]
    came = [back(up, i) for i in range(whole) for up in (1, 3)]

    @pl.loop(0, n)
    def _(d):
        @pl.when(d != me)
        def _():
            to_owner(d).wait_send()
            to_all(d).wait_send()
            to_rows(d).wait_send()

        for those, done in ((gone, "wait_send"), (came, "wait_recv")):
            here = d != me
            for it in those:
                here = jnp.logical_and(here, d != it)

            @pl.when(here)
            def _():
                for e in range(experts):
                    getattr(remote(sent.at[d, e], piece(e, d), send_sem.at[d, e], recv_sem.at[d, e], {"zero": d}), done)()

    for d, e in halves:
        to_server(d, e).wait_send()
    for slab in range(SLABS, whole * experts):
        for up in (1, 3):
            s, e = back(up, slab // experts), slab % experts
            remote(sent.at[s, e], piece(e, s), send_sem.at[s, e], recv_sem.at[s, e], {"zero": s}).wait_recv()


def deliver(ready, scale, serve, ready_out, scale_out, serve_out, sem):
    experts = ready.shape[0]
    copies = [pltpu.make_async_copy(ready.at[e], ready_out.at[e], sem.at[e]) for e in range(experts)]
    copies.append(pltpu.make_async_copy(scale, scale_out, sem.at[experts]))
    copies.append(pltpu.make_async_copy(serve, serve_out, sem.at[experts + 1]))
    for copy in copies:
        copy.start()
    for copy in copies:
        copy.wait()


def solution(mesh):
    n, banks = mesh.shape["zero"], mesh.shape["bank"]

    def local(train_down, other_down, router_weight, router_gain):
        experts, length, width = train_down.shape
        rows = length // n
        split = (experts, n, rows, width)
        dma, vmem = pltpu.SemaphoreType.DMA, pltpu.VMEM
        units = SLABS * rows // UNIT
        outs = (
            jax.ShapeDtypeStruct((experts, rows, n * width), jnp.bfloat16),
            jax.ShapeDtypeStruct((experts, rows), jnp.float32),
            jax.ShapeDtypeStruct((banks * experts, n * width), jnp.bfloat16),
        )
        anywhere = pl.BlockSpec(memory_space=pl.ANY)
        inputs = (train_down.reshape(split), other_down.reshape(split), router_weight.T, router_gain[None, :])
        results = pl.pallas_call(
            functools.partial(kernel, n, banks),
            out_shape=outs,
            in_specs=[pl.BlockSpec(memory_space=pltpu.HBM)] * 4,
            out_specs=(anywhere,) + (pl.BlockSpec(memory_space=vmem),) * 2,
            scratch_shapes=[
                vmem(split, jnp.float32),
                vmem(split, jnp.bfloat16),
                vmem((experts, width), jnp.float32),
                vmem((1, width), jnp.float32),
                vmem((n, SUB, LANES), jnp.float32),
                vmem((n, HALF, LANES), jnp.float32),
                vmem((n, HALF, LANES), jnp.float32),
                vmem((1, HALF, LANES), jnp.float32),
                vmem((n, HALF, LANES), jnp.float32),
                vmem((n, experts, rows, width), jnp.bfloat16),
                vmem((banks, n, experts, width), jnp.float32),
                vmem((2, SLABS, rows, width), jnp.float32),
                dma((2, CHUNKS + 1)),
                dma((n,)), dma((n,)), dma((n,)), dma((n,)),
                dma((n,)), dma((n,)), dma((banks,)), dma((banks,)),
                dma((n, experts)), dma((n, experts)), dma((experts + 2 * SLABS,)),
                dma((2, units)), dma((2, units)),
            ],
            compiler_params=pltpu.CompilerParams(
                collective_id=0, has_side_effects=True, vmem_limit_bytes=40 * 1024 * 1024
            ),
        )(*(pltpu.with_memory_space_constraint(a, pltpu.HBM) for a in inputs))
        ready, scale, serve = pl.pallas_call(
            deliver,
            out_shape=outs,
            in_specs=[anywhere] * 3,
            out_specs=(anywhere,) * 3,
            scratch_shapes=[dma((experts + 2,))],
            compiler_params=pltpu.CompilerParams(vmem_limit_bytes=1024 * 1024),
        )(*results)
        return ready, scale, serve.T

    in_specs = (P("bank", None, "zero"), P("bank", None, "zero"), P("zero", "bank"), P("zero"))
    out_specs = (P("bank", "zero"), P("bank", "zero"), P())
    return jax.shard_map(local, mesh=mesh, in_specs=in_specs, out_specs=out_specs, check_vma=False)
```

time: 181 us -> 101 us (0.56)
  Pallas kernels: 0 us -> 100 us
  waiting for transfers between devices: 85.1 us -> 0 us
  blocking collectives: 47.7 us -> 0 us
  starting transfers between devices: 25.6 us -> 0 us
  other arithmetic: 15.8 us -> 0 us
  local copies, waits for them, and re-layouts: 6.02 us -> 0 us
    pallas_call x0 -> x2, Pallas kernels: none -> 100 us  [the longest x1 98.2 us: local(): pl.pallas_call(functools.partial(kernel, n, banks), out_shape=outs, in_sp...]
    all_to_all x4 -> x0, waiting for transfers between devices: 85.1 us -> none  [the longest x2 81.4 us: several_exchanges(): lax.all_to_all(share, axis, split_axis=0, concat_axis=0, tiled=True)]
    all_to_all x1 -> x0, blocking collectives: 47.7 us -> none  [from_everyone(): return lax.all_to_all(copies, axis, split_axis=0, concat_axis=0, tiled=True)]
    all_to_all x4 -> x0, starting transfers between devices: 25.6 us -> none  [the longest x2 16.1 us: from_everyone(): return lax.all_to_all(copies, axis, split_axis=0, concat_axis=0, tiled=True)]
    reduce_max x2 -> x0, other arithmetic: 6.15 us -> none  [the longest x1 5.6 us: local(): scale_down = taken_together(jnp.max(jnp.abs(latest_down), axis=2), 'zero')]
    convert_element_type x2 -> x0, other arithmetic: 6 us -> none  [the longest x1 5.32 us: local(): (latest_down / jnp.expand_dims(scale_down, 2)).astype(jnp.bfloat16)]
    reshape x1 -> x0, other arithmetic: 3.6 us -> none  [laid_out(): return jnp.moveaxis(tiles, 0, dim).reshape(dims)]
    split x4 -> x0, local copies, waits for them, and re-layouts: 2.9 us -> none  [several_exchanges(): jnp.split(tiles, piece_ends(tiles.shape[cut], pieces), axis=cut)]
  transfers between devices with their start and end apart: 4 -> 0, of which waited for: 3 -> 0; matrix products, arithmetic and copies ran while one was open for 9% -> 0% of each run, Pallas kernels for 0% -> 0%
where the time goes in v3:
time: 101 us
  Pallas kernels  100 us (99%)
    pallas_call x1, Pallas kernels, local(): pl.pallas_call(functools.partial(kernel, n, banks), out_shape=outs, in_sp...  98.2 us

profile of v3, /device:TPU:41, one launch (start us, length us, event | category | flops | bytes accessed | tf_op | source)
XLA Modules:
  0.0 100.6 jit_solution(3600913367244855203)
XLA Ops:
  0.6 98.2 %shard_map.67 = (bf16[2,200,4096]{2,1,0:T(8,128)(2,1)S(1)}, f32[2,200]{1,0:T(2,128)S(1)}, bf16[16,4096]{1,0:T(8,128)(2,1)S(1)}) custom-call(f32[2,32,200,128]{3,2,1,0:T(8,128)} %bitcast.5, bf16[2,32,200,128]{3,2,1,0:T(8,128)(2,1)} %bitcast.6, f32[2,128]{1,0:T(2,128)} %bitcast.7, f32[1,128]{1,0:T(1,128)} %bitcast.8), custom_call_target="tpu_custom_call" | custom-call | tf_op jit(solution)/shard_map/pallas_call | solution.py:327
  98.8 1.8 %shard_map.68 = (bf16[2,200,4096]{2,1,0:T(8,128)(2,1)}, f32[2,200]{1,0:T(2,128)}, bf16[16,4096]{1,0:T(8,128)(2,1)}) custom-call(bf16[2,200,4096]{2,1,0:T(8,128)(2,1)S(1)} %get-tuple-element.9.ready, f32[2,200]{1,0:T(2,128)S(1)} %get-tuple-element.10.scale, bf16[16,4096]{1,0:T(8,128)(2,1)S(1)} %get-tuple-element.11.serve), custom_call_target="tpu_custom_call" | custom-call | tf_op jit(solution)/shard_map/pallas_call | solution.py:355

commit v4 on v3

--- a/solution.py
+++ b/solution.py
@@ -136,7 +136,7 @@
 
     for copy in small:
         copy.wait()
-    lines[bank, me] = (w_buf[...] * g_buf[...]).astype(jnp.bfloat16).astype(jnp.float32)
+    lines[bank, me] = (w_buf[...] * g_buf[...]).astype(jnp.bfloat16)
 
     def to_rows(d):
         return remote(lines.at[bank, me], lines.at[bank, me], row_send.at[d], row_recv.at[me], {"zero": d})
@@ -196,10 +196,8 @@
 
     halves = [(peer(up, slab // experts), slab % experts) for slab in range(SLABS, -(-SLABS // experts) * experts) for up in (1, 3)]
     whole = -(-SLABS // experts)
-    for up in (1, 3):
-        for i in range(whole):
-            known(peer(up, i))
     for d, e in halves:
+        known(d)
         narrow(d, e, x_buf[e, d], inv[d])
     was = peer(1, whole)
     known(was)
@@ -219,13 +217,14 @@
 
     was = lax.fori_loop(whole + 1, 4, lambda i, was: step(3, i, step(1, i, was)), was)
 
+    was = lax.fori_loop(0, 4, lambda i, was: step(2, i, was), was)
+    was = lax.fori_loop(4, plane, lambda i, was: step(2, i, step(3, i, step(1, i, was))), was)
+
     line(bank, across, 0).wait()
     for k, b in enumerate(beside):
         line(bank, b, 1 + k).start()
         line(across, b, row_of + k).start()
 
-    was = lax.fori_loop(0, 4, lambda i, was: step(2, i, was), was)
-    was = lax.fori_loop(4, plane, lambda i, was: step(2, i, step(3, i, step(1, i, was))), was)
     was = lax.fori_loop(1, plane, lambda i, was: step(0, i, was), was)
     for e in range(experts):
         to_server(was, e).start()
@@ -265,11 +264,8 @@
         remote(lines.at[b], lines.at[b], line_send.at[k], line_recv.at[k], {"bank": b}).wait_recv()
         remote(lines.at[far], lines.at[far], line_send.at[row_of + k - 1], line_recv.at[row_of + k - 1], {"bank": b}).wait_recv()
     for s in range(n):
-        columns = jnp.concatenate([lines[b, s] for b in range(banks)], axis=0)
+        columns = jnp.concatenate([lines[b, s].astype(jnp.float32) for b in range(banks)], axis=0)
         serve[:, s * LANES : (s + 1) * LANES] = columns.astype(jnp.bfloat16)
-
-    gone = [peer(up, i) for i in range(whole) for up in (1, 3)]
-    came = [back(up, i) for i in range(whole) for up in (1, 3)]
 
     @pl.loop(0, n)
     def _(d):
@@ -279,22 +275,28 @@
             to_all(d).wait_send()
             to_rows(d).wait_send()
 
-        for those, done in ((gone, "wait_send"), (came, "wait_recv")):
-            here = d != me
-            for it in those:
-                here = jnp.logical_and(here, d != it)
-
-            @pl.when(here)
-            def _():
-                for e in range(experts):
-                    getattr(remote(sent.at[d, e], piece(e, d), send_sem.at[d, e], recv_sem.at[d, e], {"zero": d}), done)()
-
-    for d, e in halves:
-        to_server(d, e).wait_send()
+    for i in range(SLABS // experts):
+        for up in (1, 3):
+            known(peer(up, i))
+
     for slab in range(SLABS, whole * experts):
         for up in (1, 3):
-            s, e = back(up, slab // experts), slab % experts
+            d, s, e = peer(up, slab // experts), back(up, slab // experts), slab % experts
+            to_server(d, e).wait_send()
             remote(sent.at[s, e], piece(e, s), send_sem.at[s, e], recv_sem.at[s, e], {"zero": s}).wait_recv()
+
+    def over(up, i):
+        d, s = peer(up, i), back(up, i)
+        for e in range(experts):
+            to_server(d, e).wait_send()
+            remote(sent.at[s, e], piece(e, s), send_sem.at[s, e], recv_sem.at[s, e], {"zero": s}).wait_recv()
+
+    for lo, hi, ups in ((whole, 4, (1, 3)), (0, 4, (2,)), (4, plane, (1, 3, 2)), (1, plane, (0,))):
+
+        @pl.loop(lo, hi)
+        def _(i):
+            for up in ups:
+                over(up, i)
 
 
 def deliver(ready, scale, serve, ready_out, scale_out, serve_out, sem):
@@ -340,7 +342,7 @@
                 vmem((1, HALF, LANES), jnp.float32),
                 vmem((n, HALF, LANES), jnp.float32),
                 vmem((n, experts, rows, width), jnp.bfloat16),
-                vmem((banks, n, experts, width), jnp.float32),
+                vmem((banks, n, experts, width), jnp.bfloat16),
                 vmem((2, SLABS, rows, width), jnp.float32),
                 dma((2, CHUNKS + 1)),
                 dma((n,)), dma((n,)), dma((n,)), dma((n,)),

time: 101 us -> 99.4 us (0.984); the launches traced: 101 us -> 97.5 us
  Pallas kernels: 100 us -> 96.8 us
    pallas_call x1, Pallas kernels: 98.2 us -> 95.1 us  [local(): pl.pallas_call(functools.partial(kernel, n, banks), out_shape=outs, in_sp...]
where the time goes in v4:
time: 99.4 us; the launch traced here: 97.5 us
  Pallas kernels  96.8 us (97%)
    pallas_call x1, Pallas kernels, local(): pl.pallas_call(functools.partial(kernel, n, banks), out_shape=outs, in_sp...  95.1 us

profile of v4, /device:TPU:41, one launch (start us, length us, event | category | flops | bytes accessed | tf_op | source)
XLA Modules:
  0.0 97.5 jit_solution(1169016563789507788)
XLA Ops:
  0.6 95.1 %shard_map.67 = (bf16[2,200,4096]{2,1,0:T(8,128)(2,1)S(1)}, f32[2,200]{1,0:T(2,128)S(1)}, bf16[16,4096]{1,0:T(8,128)(2,1)S(1)}) custom-call(f32[2,32,200,128]{3,2,1,0:T(8,128)} %bitcast.5, bf16[2,32,200,128]{3,2,1,0:T(8,128)(2,1)} %bitcast.6, f32[2,128]{1,0:T(2,128)} %bitcast.7, f32[1,128]{1,0:T(1,128)} %bitcast.8), custom_call_target="tpu_custom_call" | custom-call | tf_op jit(solution)/shard_map/pallas_call | solution.py:329
  95.7 1.8 %shard_map.68 = (bf16[2,200,4096]{2,1,0:T(8,128)(2,1)}, f32[2,200]{1,0:T(2,128)}, bf16[16,4096]{1,0:T(8,128)(2,1)}) custom-call(bf16[2,200,4096]{2,1,0:T(8,128)(2,1)S(1)} %get-tuple-element.9.ready, f32[2,200]{1,0:T(2,128)S(1)} %get-tuple-element.10.scale, bf16[16,4096]{1,0:T(8,128)(2,1)S(1)} %get-tuple-element.11.serve), custom_call_target="tpu_custom_call" | custom-call | tf_op jit(solution)/shard_map/pallas_call | solution.py:357

commit v5 on v4

--- a/solution.py
+++ b/solution.py
@@ -14,7 +14,6 @@
 CHUNKS = 8
 UNIT = 40
 SLABS = 2
-EARLY, PACE = 6, 1
 DURING = 6
 
 
@@ -41,6 +40,10 @@
         z, x, c = lax.rem(me // plane + up, PLANES), lax.rem(me % plane // 2 + i // 2, plane // 2), lax.rem(me + i, 2)
         return z * plane + x * 2 + c
 
+    planes = [lax.rem(me // plane + up, PLANES) * plane for up in range(PLANES)]
+    places = [lax.rem(me % plane // 2 + i, plane // 2) * 2 for i in range(plane // 2)]
+    cores = [lax.rem(me + i, 2) for i in range(2)]
+
     def back(up, i):
         z, x, c = lax.rem(me // plane + PLANES - up, PLANES), lax.rem(me % plane // 2 + plane // 2 - i // 2, plane // 2), lax.rem(me + i, 2)
         return z * plane + x * 2 + c
@@ -55,13 +58,11 @@
 
     def others(body, ups=(2, 1, 3, 0)):
         for up in ups:
-
-            @pl.loop(1 if up == 0 else 0, plane)
-            def _(i):
-                body(peer(up, i))
+            for i in range(1 if up == 0 else 0, plane):
+                body(planes[up] + places[i // 2] + cores[i % 2])
 
     def chunk(k):
-        return lax.rem(me // per + plane // per + k, CHUNKS)
+        return lax.rem(me // plane * (plane // per) + plane // per + k, CHUNKS)
 
     def load(k):
         g = chunk(k)
@@ -112,27 +113,21 @@
                 top = jnp.max(jnp.abs(x).reshape(tiles, SUB, LANES), axis=2, keepdims=True)
                 for t in range(tiles):
                     tile = jnp.where(lane == e * tiles + t, top[t], tile)
-            loose[d] = tile
-
-    pl.loop(0, EARLY)(maxima)
-    pl.semaphore_wait(barrier, n - 1 + row_of)
-
-    @pl.loop(EARLY, CHUNKS)
-    def _(g):
-        maxima(g)
-        for way in range(2):
-            for k in range(PACE):
-                raw(way, (g - EARLY) * PACE + k).start()
-
-    for d in range(n):
-        part[d] = packed(loose[d])
+            loose[j] = tile
+        for j in range(per):
+            part[chunk(k) * per + j] = packed(loose[j])
 
     def to_owner(d):
         return remote(part.at[d], heard.at[me], max_send.at[d], max_recv.at[me], {"zero": d})
 
-    others(lambda d: to_owner(d).start())
-
-    raws((CHUNKS - EARLY) * PACE, (CHUNKS - EARLY) * PACE + DURING)
+    apart = CHUNKS - plane // per
+    pl.loop(0, apart)(maxima)
+    pl.semaphore_wait(barrier, n - 1 + row_of)
+    others(lambda d: to_owner(d).start(), (2, 1, 3))
+    pl.loop(apart, CHUNKS)(maxima)
+    others(lambda d: to_owner(d).start(), (0,))
+
+    raws(0, DURING)
 
     for copy in small:
         copy.wait()
@@ -169,7 +164,7 @@
 
     others(lambda d: to_all(d).start(), (1, 3, 2, 0))
 
-    raws((CHUNKS - EARLY) * PACE + DURING, SLABS * units)
+    raws(DURING, SLABS * units)
 
     def piece(e, at):
         return ready.at[e, :, pl.ds(pl.multiple_of(at * LANES, LANES), LANES)]
@@ -218,7 +213,13 @@
     was = lax.fori_loop(whole + 1, 4, lambda i, was: step(3, i, step(1, i, was)), was)
 
     was = lax.fori_loop(0, 4, lambda i, was: step(2, i, was), was)
-    was = lax.fori_loop(4, plane, lambda i, was: step(2, i, step(3, i, step(1, i, was))), was)
+    high = me // plane
+    first = jnp.where(high == 0, 2, PLANES - high)
+    second = jnp.where(high == 0, 1, jnp.where(high == 2, 3, 2))
+    third = jnp.where(high == 1, 1, jnp.where(high == 2, 1, 3))
+    was = lax.fori_loop(4, 6, lambda i, was: step(third, i, step(second, i, step(first, i, was))), was)
+    was = lax.fori_loop(6, plane, lambda i, was: step(second, i, step(first, i, was)), was)
+    was = lax.fori_loop(6, plane, lambda i, was: step(third, i, was), was)
 
     line(bank, across, 0).wait()
     for k, b in enumerate(beside):
@@ -336,7 +337,7 @@
                 vmem(split, jnp.bfloat16),
                 vmem((experts, width), jnp.float32),
                 vmem((1, width), jnp.float32),
-                vmem((n, SUB, LANES), jnp.float32),
+                vmem((n // CHUNKS, SUB, LANES), jnp.float32),
                 vmem((n, HALF, LANES), jnp.float32),
                 vmem((n, HALF, LANES), jnp.float32),
                 vmem((1, HALF, LANES), jnp.float32),

time: 99.4 us -> 96.3 us (0.969); the launches traced: 97.5 us -> 95.5 us
  Pallas kernels: 96.8 us -> 94.9 us
    pallas_call x1, Pallas kernels: 95.1 us -> 93.1 us  [local(): pl.pallas_call(functools.partial(kernel, n, banks), out_shape=outs, in_sp...]
where the time goes in v5:
time: 96.3 us; the launch traced here: 95.5 us
  Pallas kernels  94.9 us (99%)
    pallas_call x1, Pallas kernels, local(): pl.pallas_call(functools.partial(kernel, n, banks), out_shape=outs, in_sp...  93.1 us

profile of v5, /device:TPU:41, one launch (start us, length us, event | category | flops | bytes accessed | tf_op | source)
XLA Modules:
  0.0 95.5 jit_solution(15097475532205846807)
XLA Ops:
  0.6 93.1 %shard_map.67 = (bf16[2,200,4096]{2,1,0:T(8,128)(2,1)S(1)}, f32[2,200]{1,0:T(2,128)S(1)}, bf16[16,4096]{1,0:T(8,128)(2,1)S(1)}) custom-call(f32[2,32,200,128]{3,2,1,0:T(8,128)} %bitcast.5, bf16[2,32,200,128]{3,2,1,0:T(8,128)(2,1)} %bitcast.6, f32[2,128]{1,0:T(2,128)} %bitcast.7, f32[1,128]{1,0:T(1,128)} %bitcast.8), custom_call_target="tpu_custom_call" | custom-call | tf_op jit(solution)/shard_map/pallas_call | solution.py:330
  93.7 1.8 %shard_map.68 = (bf16[2,200,4096]{2,1,0:T(8,128)(2,1)}, f32[2,200]{1,0:T(2,128)}, bf16[16,4096]{1,0:T(8,128)(2,1)}) custom-call(bf16[2,200,4096]{2,1,0:T(8,128)(2,1)S(1)} %get-tuple-element.9.ready, f32[2,200]{1,0:T(2,128)S(1)} %get-tuple-element.10.scale, bf16[16,4096]{1,0:T(8,128)(2,1)S(1)} %get-tuple-element.11.serve), custom_call_target="tpu_custom_call" | custom-call | tf_op jit(solution)/shard_map/pallas_call | solution.py:358

commit v6 on v5

--- a/solution.py
+++ b/solution.py
@@ -12,9 +12,9 @@
 HALF = SUB // 2
 PLANES = 4
 CHUNKS = 8
-UNIT = 40
+UNIT = 200
 SLABS = 2
-DURING = 6
+DURING = 1
 
 
 def remote(src, dst, send, recv, where):
@@ -162,7 +162,7 @@
     def to_all(d):
         return remote(told.at[0], inv.at[me], inv_send.at[d], inv_recv.at[me], {"zero": d})
 
-    others(lambda d: to_all(d).start(), (1, 3, 2, 0))
+    others(lambda d: to_all(d).start(), (1, 3, 0, 2))
 
     raws(DURING, SLABS * units)
 
@@ -213,6 +213,7 @@
     was = lax.fori_loop(whole + 1, 4, lambda i, was: step(3, i, step(1, i, was)), was)
 
     was = lax.fori_loop(0, 4, lambda i, was: step(2, i, was), was)
+    was = lax.fori_loop(1, 4, lambda i, was: step(0, i, was), was)
     high = me // plane
     first = jnp.where(high == 0, 2, PLANES - high)
     second = jnp.where(high == 0, 1, jnp.where(high == 2, 3, 2))
@@ -221,12 +222,13 @@
     was = lax.fori_loop(6, plane, lambda i, was: step(second, i, step(first, i, was)), was)
     was = lax.fori_loop(6, plane, lambda i, was: step(third, i, was), was)
 
+    was = lax.fori_loop(4, plane, lambda i, was: step(0, i, was), was)
+
     line(bank, across, 0).wait()
     for k, b in enumerate(beside):
         line(bank, b, 1 + k).start()
         line(across, b, row_of + k).start()
 
-    was = lax.fori_loop(1, plane, lambda i, was: step(0, i, was), was)
     for e in range(experts):
         to_server(was, e).start()
 

time: 96.3 us -> 95.7 us (level)
  no operation moved by 1% of the time
where the time goes in v6:
time: 95.7 us; the launch traced here: 94.7 us
  Pallas kernels  94.1 us (98%)
    pallas_call x1, Pallas kernels, local(): pl.pallas_call(functools.partial(kernel, n, banks), out_shape=outs, in_sp...  92.3 us

profile of v6, /device:TPU:41, one launch (start us, length us, event | category | flops | bytes accessed | tf_op | source)
XLA Modules:
  0.0 94.7 jit_solution(1771772690853520084)
XLA Ops:
  0.6 92.3 %shard_map.67 = (bf16[2,200,4096]{2,1,0:T(8,128)(2,1)S(1)}, f32[2,200]{1,0:T(2,128)S(1)}, bf16[16,4096]{1,0:T(8,128)(2,1)S(1)}) custom-call(f32[2,32,200,128]{3,2,1,0:T(8,128)} %bitcast.5, bf16[2,32,200,128]{3,2,1,0:T(8,128)(2,1)} %bitcast.6, f32[2,128]{1,0:T(2,128)} %bitcast.7, f32[1,128]{1,0:T(1,128)} %bitcast.8), custom_call_target="tpu_custom_call" | custom-call | tf_op jit(solution)/shard_map/pallas_call | solution.py:332
  93.0 1.8 %shard_map.68 = (bf16[2,200,4096]{2,1,0:T(8,128)(2,1)}, f32[2,200]{1,0:T(2,128)}, bf16[16,4096]{1,0:T(8,128)(2,1)}) custom-call(bf16[2,200,4096]{2,1,0:T(8,128)(2,1)S(1)} %get-tuple-element.9.ready, f32[2,200]{1,0:T(2,128)S(1)} %get-tuple-element.10.scale, bf16[16,4096]{1,0:T(8,128)(2,1)S(1)} %get-tuple-element.11.serve), custom_call_target="tpu_custom_call" | custom-call | tf_op jit(solution)/shard_map/pallas_call | solution.py:360

commit v7 on v6

--- a/solution.py
+++ b/solution.py
@@ -219,8 +219,8 @@
     second = jnp.where(high == 0, 1, jnp.where(high == 2, 3, 2))
     third = jnp.where(high == 1, 1, jnp.where(high == 2, 1, 3))
     was = lax.fori_loop(4, 6, lambda i, was: step(third, i, step(second, i, step(first, i, was))), was)
-    was = lax.fori_loop(6, plane, lambda i, was: step(second, i, step(first, i, was)), was)
-    was = lax.fori_loop(6, plane, lambda i, was: step(third, i, was), was)
+    was = lax.fori_loop(6, plane, lambda i, was: step(first, i, was), was)
+    was = lax.fori_loop(6, plane, lambda i, was: step(third, i, step(second, i, was)), was)
 
     was = lax.fori_loop(4, plane, lambda i, was: step(0, i, was), was)
 

time: 95.7 us -> 95.6 us (level)
  the two profiles are of different devices: /device:TPU:41 before, /device:TPU:65 now
where the time goes in v7:
time: 95.6 us
  Pallas kernels  94.9 us (99%)
    pallas_call x1, Pallas kernels, local(): pl.pallas_call(functools.partial(kernel, n, banks), out_shape=outs, in_sp...  93.1 us

profile of v7, /device:TPU:65, one launch (start us, length us, event | category | flops | bytes accessed | tf_op | source)
XLA Modules:
  0.0 95.6 jit_solution(14467439744828447016)
XLA Ops:
  0.6 93.1 %shard_map.67 = (bf16[2,200,4096]{2,1,0:T(8,128)(2,1)S(1)}, f32[2,200]{1,0:T(2,128)S(1)}, bf16[16,4096]{1,0:T(8,128)(2,1)S(1)}) custom-call(f32[2,32,200,128]{3,2,1,0:T(8,128)} %bitcast.5, bf16[2,32,200,128]{3,2,1,0:T(8,128)(2,1)} %bitcast.6, f32[2,128]{1,0:T(2,128)} %bitcast.7, f32[1,128]{1,0:T(1,128)} %bitcast.8), custom_call_target="tpu_custom_call" | custom-call | tf_op jit(solution)/shard_map/pallas_call | solution.py:332
  93.8 1.8 %shard_map.68 = (bf16[2,200,4096]{2,1,0:T(8,128)(2,1)}, f32[2,200]{1,0:T(2,128)}, bf16[16,4096]{1,0:T(8,128)(2,1)}) custom-call(bf16[2,200,4096]{2,1,0:T(8,128)(2,1)S(1)} %get-tuple-element.9.ready, f32[2,200]{1,0:T(2,128)S(1)} %get-tuple-element.10.scale, bf16[16,4096]{1,0:T(8,128)(2,1)S(1)} %get-tuple-element.11.serve), custom_call_target="tpu_custom_call" | custom-call | tf_op jit(solution)/shard_map/pallas_call | solution.py:360
